TPU v7x, 32 devices: a whole 2x2x4 slice. The times are simulated.
32 devices in a mesh: section: 4 (over y, core), tp: 8 (over z, x).
Axes of the slice: x: 2, y: 2, z: 4, core: 2. Of those that a mesh axis runs over, the one named last changes fastest.
Arguments:
- embedded: bfloat16 [384, 4096], P('tp'), may hold values from -20 to 20
- previous_out: bfloat16 [4, 384, 4096], P('section', 'tp'), may hold values from -20 to 20
- top_grad: bfloat16 [384, 4096], P('tp'), may hold values from -6 to 6
- grad_out: bfloat16 [4, 384, 4096], P('section', 'tp'), may hold values from -6 to 6
- saved_input: bfloat16 [4, 384, 4096], P('section', 'tp'), may hold values from -20 to 20
- saved_qkv: bfloat16 [4, 384, 3, 2048], P('section', None, None, 'tp'), may hold values from -64 to 64
- norm_gain: float32 [4, 2, 4096], P('section'), may hold values from 0.1 to 1.9
- qkv_weight: bfloat16 [4, 2, 4096, 3, 2048], P('section', None, None, None, 'tp'), may hold values from -4 to 4
- out_weight: bfloat16 [4, 2, 2048, 4096], P('section', None, 'tp'), may hold values from -0.125 to 0.125
- modality: int32 [4, 2, 384], P('section'), may hold values from 0 to 1, as said below
- documents: int32 [4, 2, 384], P('section'), may hold values from 0 to 3, never falling along the last dimension, each value on 1 to 192 neighbouring positions
Outputs:
- forward_out: bfloat16 [4, 384, 4096], P('section', 'tp')
- backward_out: bfloat16 [4, 384, 4096], P('section', 'tp')
Inputs may be any that keep to these rules, and one draw needn't show every extreme that they name: `modality`: 0 marks a text token and 1 an image token; image tokens come in runs of positions, and both modalities occur in every micro-batch. `documents`: document numbers start at 0 and never fall along the positions of a micro-batch.
All inputs are finite; a program needn't handle non-finite values.
Results may differ from a plain program's by a relative error of at most 0.014.
Values may be sent and summed in bfloat16 or wider, within the bound.
A program may use at most 128 MiB of HBM per device.

v0:
```python
import math

import jax
import jax.numpy as jnp
from jax import lax
from jax.sharding import PartitionSpec as P

HEAD_DIM = 128


EPSILON = 1e-05


def from_behind(block, axis, distance):
    devices = range(lax.axis_size(axis))
    route = [(i - distance, i) for i in devices if i - distance in devices]
    return lax.ppermute(block, axis, route)


def contract(rows, weights, side):
    return lax.dot_general(
        rows, weights, (((1,), (side,)), ((), ())), preferred_element_type=jnp.float32
    )


def selected(rows, labels, weights, side):
    first = contract(rows, weights[0], side)
    second = contract(rows, weights[1], side)
    return jnp.where(labels[:, None] == 0, first, second)


def project(rows, labels, weights, side):
    result = selected(rows, labels, weights, side)
    return result


def term_source(rows, labels, weights, side):

    def piece(first, row_count):
        return selected(rows, labels, weights, side)

    return piece


def gain_rows(gains, labels):
    return jnp.where(labels[:, None] == 0, gains[0][None, :], gains[1][None, :])


def probabilities(queries, keys, documents_row):
    length = queries.shape[0]
    scores = jnp.einsum(
        "thd,shd->hts", queries, keys, preferred_element_type=jnp.float32
    ) / math.sqrt(HEAD_DIM)
    position = jnp.arange(length, dtype=jnp.int32)
    allowed = (position[None, :] <= position[:, None]) & (
        documents_row[:, None] == documents_row[None, :]
    )
    scores = jnp.where(allowed[None, :, :], scores, -jnp.inf)
    highest = jnp.max(scores, axis=-1, keepdims=True)
    weights = jnp.exp(scores - highest)
    return weights / jnp.sum(weights, axis=-1, keepdims=True)


def forward_attention(normed_all, labels, documents_row, w_project, heads_here):
    length = normed_all.shape[0]
    projected = project(normed_all, labels, w_project, 0).astype(jnp.bfloat16)
    projected = projected.reshape(length, 3, heads_here, HEAD_DIM)
    probs = probabilities(projected[:, 0], projected[:, 1], documents_row).astype(jnp.bfloat16)
    attended = jnp.einsum(
        "hts,shd->thd", probs, projected[:, 2], preferred_element_type=jnp.float32
    )
    return attended.astype(jnp.bfloat16).reshape(length, heads_here * HEAD_DIM)


def backward_attention(upstream_all, labels, documents_row, w_output, saved, heads_here):
    length = upstream_all.shape[0]
    grad_attended = project(upstream_all, labels, w_output, 1).astype(jnp.bfloat16)
    grad_attended = grad_attended.reshape(length, heads_here, HEAD_DIM)
    stored = saved.reshape(length, 3, heads_here, HEAD_DIM)
    queries = stored[:, 0]
    keys = stored[:, 1]
    values = stored[:, 2]
    probs_back = probabilities(queries, keys, documents_row)
    rounded = probs_back.astype(jnp.bfloat16)
    grad_values = jnp.einsum(
        "hts,thd->shd", rounded, grad_attended, preferred_element_type=jnp.float32
    ).astype(jnp.bfloat16)
    grad_probs = jnp.einsum(
        "thd,shd->hts", grad_attended, values, preferred_element_type=jnp.float32
    )
    delta = jnp.sum(probs_back * grad_probs, axis=-1, keepdims=True)
    grad_scores = (probs_back * (grad_probs - delta) / math.sqrt(HEAD_DIM)).astype(jnp.bfloat16)
    grad_queries = jnp.einsum(
        "hts,shd->thd", grad_scores, keys, preferred_element_type=jnp.float32
    ).astype(jnp.bfloat16)
    grad_keys = jnp.einsum(
        "hts,thd->shd", grad_scores, queries, preferred_element_type=jnp.float32
    ).astype(jnp.bfloat16)
    return jnp.stack([grad_queries, grad_keys, grad_values], axis=1).reshape(
        length, 3 * heads_here * HEAD_DIM
    )


def body(
    embedded,
    previous_out,
    top_grad,
    grad_out,
    saved_input,
    saved_qkv,
    norm_gain,
    qkv_weight,
    out_weight,
    modality,
    documents,
):
    section = lax.axis_index("section")
    arrived = from_behind(previous_out[0], "section", 1)
    returned = from_behind(grad_out[0], "section", -1)
    inputs = jnp.where(section == 0, embedded, arrived)
    upstream = jnp.where(section == lax.axis_size("section") - 1, top_grad, returned)
    local = inputs.shape[0]
    width = inputs.shape[1]
    offset = lax.axis_index("tp") * local
    labels_fwd = modality[0, 0]
    labels_back = modality[0, 1]
    documents_fwd = documents[0, 0]
    documents_back = documents[0, 1]
    gains = norm_gain[0]
    heads_here = qkv_weight.shape[-1] // HEAD_DIM
    w_project = qkv_weight[0].reshape(2, width, 3 * heads_here * HEAD_DIM)
    w_output = out_weight[0]
    own_fwd = lax.dynamic_slice_in_dim(labels_fwd, offset, local, 0)
    own_back = lax.dynamic_slice_in_dim(labels_back, offset, local, 0)
    forward_rows = inputs.astype(jnp.float32)
    inverse = lax.rsqrt(jnp.mean(forward_rows * forward_rows, axis=-1, keepdims=True) + EPSILON)
    normed = (forward_rows * inverse * gain_rows(gains, own_fwd)).astype(jnp.bfloat16)
    normed_all, upstream_all = (
        lax.all_gather(normed, "tp", axis=0, tiled=True),
        lax.all_gather(upstream, "tp", axis=0, tiled=True),
    )
    attended = forward_attention(normed_all, labels_fwd, documents_fwd, w_project, heads_here)
    grads_flat = backward_attention(
        upstream_all, labels_back, documents_back, w_output, saved_qkv[0], heads_here
    )
    forward_piece = term_source(attended, labels_fwd, w_output, 0)
    backward_piece = term_source(grads_flat, labels_back, w_project, 1)
    first = jnp.int32(0)
    summed = lax.psum_scatter(
        jnp.concatenate(
            [
                forward_piece(first, local * lax.axis_size("tp")),
                backward_piece(first, local * lax.axis_size("tp")),
            ],
            axis=1,
        ).astype(jnp.bfloat16),
        "tp",
        scatter_dimension=0,
        tiled=True,
    ).astype(jnp.float32)
    mixed = summed[:, :width]
    grad_normed = summed[:, width:]
    forward_out = (forward_rows + mixed).astype(jnp.bfloat16)
    back_rows = saved_input[0].astype(jnp.float32)
    inverse_back = lax.rsqrt(jnp.mean(back_rows * back_rows, axis=-1, keepdims=True) + EPSILON)
    scaled = grad_normed * gain_rows(gains, own_back)
    correction = jnp.mean(scaled * back_rows, axis=-1, keepdims=True)
    norm_grad = (
        inverse_back * scaled - back_rows * inverse_back * inverse_back * inverse_back * correction
    )
    backward_out = (upstream.astype(jnp.float32) + norm_grad).astype(jnp.bfloat16)
    return (forward_out[None], backward_out[None])


def solution(mesh):
    placed = (
        P("tp", None),
        P("section", "tp", None),
        P("tp", None),
        P("section", "tp", None),
        P("section", "tp", None),
        P("section", None, None, "tp"),
        P("section", None, None),
        P("section", None, None, None, "tp"),
        P("section", None, "tp", None),
        P("section", None, None),
        P("section", None, None),
    )
    return jax.shard_map(
        body,
        mesh=mesh,
        in_specs=placed,
        out_specs=(P("section", "tp", None), P("section", "tp", None)),
        check_vma=False,
    )
```

profile of v0, /device:TPU:0, one launch (start us, length us, event | category | flops | bytes accessed | tf_op | source)
XLA Modules:
  0.0 293.4 jit_solution(18333268112336202084)
XLA Ops:
  7.3 1.4 collective-permute-start.1
  8.7 2.5 collective-permute-done.1
  12.1 8.8 %collective-permute-start = (bf16[48,4096]{1,0:T(8,128)(2,1)S(1)}, bf16[48,4096]{1,0:T(8,128)(2,1)S(1)}, u32[]{:S(2)}, u32[]{:S(2)}) collective-permute-start(bf16[48,4096]{1,0:T(8,128)(2,1)S(1)} %bitcast.151), channel_id=1, source_target_pairs={{0,8},{8,16},{16,24},{1,9},{9,17},{17,25},{2,10},{10,18},{18,26},{... | collective-permute-start | bytes 1179656 | tf_op jit(solution)/shard_map/ppermute | solution.py:17
  23.5 10.2 %fusion.74 = (bf16[1,1,4096,3,256]{4,2,3,1,0:T(8,128)(2,1)}, bf16[1,1,4096,3,256]{4,2,3,1,0:T(8,128)(2,1)}) fusion(bf16[1,2,4096,3,256]{4,2,3,1,0:T(8,128)(2,1)} %param.18), kind=kLoop, calls=%fused_computation.102 | loop fusion | bytes 25165824 | tf_op jit(solution)/shard_map/slice | solution.py:28
  33.6 8.8 %copy.46 = bf16[1,1,4096,3,256]{2,4,3,1,0:T(8,128)(2,1)} copy(bf16[1,1,4096,3,256]{4,2,3,1,0:T(8,128)(2,1)} %get-tuple-element.11) | data formatting | bytes 12582912
  42.4 8.8 %copy.47 = bf16[1,1,4096,3,256]{2,4,3,1,0:T(8,128)(2,1)} copy(bf16[1,1,4096,3,256]{4,2,3,1,0:T(8,128)(2,1)} %get-tuple-element.10) | data formatting | bytes 12582912
  52.5 1.7 fusion.78
  54.1 24.8 %all-gather.5.cloned.1.call-done = bf16[384,4096]{1,0:T(8,128)(2,1)} async-done(((bf16[48,4096]{1,0:T(8,128)(2,1)}), bf16[384,4096]{1,0:T(8,128)(2,1)}) %all-gather.5.cloned.1.call-update) | async-done | bytes 3145744 | tf_op jit(solution)/shard_map/all_gather | solution.py:140
  79.0 4.0 %fusion.3 = bf16[384,256]{0,1:T(8,128)(2,1)S(1)} fusion(bf16[384,4096]{1,0:T(8,128)(2,1)} %all-gather.5.cloned.1.call-done, bf16[1,2,256,4096]{3,2,1,0:T(8,128)(2,1)} %param.19), kind=kOutput, calls=%fused_computation.6 | convolution fusion | flops 805306368 | bytes 5439488 | tf_op jit(solution)/shard_map/dot_general | solution.py:21
  83.0 3.2 %fusion.28 = bf16[384,256]{0,1:T(8,128)(2,1)S(1)} fusion(bf16[384,256]{0,1:T(8,128)(2,1)S(1)} %fusion.3, bf16[384,4096]{1,0:T(8,128)(2,1)} %all-gather.5.cloned.1.call-done, bf16[1,2,256,4096]{3,2,1,0:T(8,128)(2,1)S(1)} %copy-done.2, pred[384]{0:T(512)(128)(4,1)S(1)} %get-tuple-element.5), kind=kOutput, calls=%fused_computation.39 | convolution fusion | flops 805404672 | bytes 5636608 | tf_op jit(solution)/shard_map/dot_general | solution.py:21
  86.5 2.2 fusion.33
  88.7 2.3 fusion.31
  91.0 2.4 fusion.32
  93.4 47.1 %all-gather.3.cloned.1.call-done = bf16[384,4096]{1,0:T(8,128)(2,1)} async-done(((bf16[48,4096]{1,0:T(8,128)(2,1)}), bf16[384,4096]{1,0:T(8,128)(2,1)}) %all-gather.3.cloned.1.call-update) | async-done | bytes 3145744 | tf_op jit(solution)/shard_map/all_gather | solution.py:139
  140.5 6.5 %fusion.80 = bf16[384,768]{1,0:T(8,128)(2,1)S(1)} fusion(bf16[384,4096]{1,0:T(8,128)(2,1)} %all-gather.3.cloned.1.call-done, bf16[4096,768]{0,1:T(8,128)(2,1)} %bitcast.124), kind=kOutput, calls=%fused_computation.108 | convolution fusion | flops 2415919104 | bytes 10027008 | tf_op jit(solution)/shard_map/dot_general | solution.py:21
  147.0 2.7 fusion.23
  152.0 2.8 fusion.8
  154.8 3.0 %select_convert_fusion.1 = bf16[384,4096]{1,0:T(8,128)(2,1)S(1)} fusion(bf16[384,4096]{1,0:T(8,128)(2,1)S(1)} %fusion.8, bf16[384,256]{0,1:T(8,128)(2,1)S(1)} %bitcast.141, pred[384]{0:T(512)(128)(4,1)S(1)} %get-tuple-element.4, bf16[1,2,256,4096]{3,2,1,0:T(8,128)(2,1)} %param.19), kind=kOutput, calls=%fused_computation.5 | convolution fusion | flops 806879232 | bytes 8585600 | tf_op jit(solution)/shard_map/dot_general | solution.py:21
  157.9 2.9 fusion.81
  160.8 2.9 select_convert_fusion
  163.7 3.4 %pad_maximum_fusion = bf16[384,8192]{1,0:T(8,128)(2,1)} fusion(bf16[384,4096]{1,0:T(8,128)(2,1)S(1)} %select_convert_fusion, bf16[384,4096]{1,0:T(8,128)(2,1)S(1)} %select_convert_fusion.1), kind=kLoop, calls=%fused_computation.3 | loop fusion | flops 12582912 | bytes 12582912 | tf_op jit(solution)/shard_map/concatenate | solution.py:150
  167.2 116.7 %reduce-scatter.2.cloned.1.call-done = bf16[48,8192]{1,0:T(8,128)(2,1)} async-done(((bf16[384,8192]{1,0:T(8,128)(2,1)}), bf16[48,8192]{1,0:T(8,128)(2,1)}) %reduce-scatter.2.cloned.1.call-update) | async-done | bytes 786448 | tf_op jit(solution)/shard_map/reduce_scatter | solution.py:149
  283.9 1.2 convert_element_type.79
  285.6 1.3 fusion.57
  (68 shorter events, 7.9 us)
Async XLA Ops:
  7.2 4.9 %copy-start.11 = (bf16[1,48,4096]{2,1,0:T(8,128)(2,1)S(1)}, bf16[1,48,4096]{2,1,0:T(8,128)(2,1)}, u32[]{:S(2)}) copy-start(bf16[1,48,4096]{2,1,0:T(8,128)(2,1)} %param.12) | copy-start | bytes 1179652
  7.2 13.7 %copy-start.7 = (f32[1,2,4096]{2,1,0:T(2,128)S(1)}, f32[1,2,4096]{2,1,0:T(2,128)}, u32[]{:S(2)}) copy-start(f32[1,2,4096]{2,1,0:T(2,128)} %param.17) | copy-start | bytes 98308
  7.2 13.7 %copy-start.8 = (s32[1,2,384]{2,1,0:T(2,128)S(1)}, s32[1,2,384]{2,1,0:T(2,128)}, u32[]{:S(2)}) copy-start(s32[1,2,384]{2,1,0:T(2,128)} %param.20) | copy-start | bytes 9220
  7.2 15.0 %copy-start.4 = (bf16[48,4096]{1,0:T(8,128)(2,1)S(1)}, bf16[48,4096]{1,0:T(8,128)(2,1)}, u32[]{:S(2)}) copy-start(bf16[48,4096]{1,0:T(8,128)(2,1)} %param.11) | copy-start | bytes 1179652
  7.2 71.8 %all-gather.5.cloned.1.call-start = ((), (), s32[]{:S(2)}) async-start(), calls=%async_computation.2 | async-start | bytes 3538944 | tf_op jit(solution)/shard_map/all_gather | solution.py:140
  7.3 4.0 %collective-permute-start.1 = (bf16[48,4096]{1,0:T(8,128)(2,1)}, bf16[48,4096]{1,0:T(8,128)(2,1)S(1)}, u32[]{:S(2)}, u32[]{:S(2)}) collective-permute-start(bf16[48,4096]{1,0:T(8,128)(2,1)} %bitcast.150), channel_id=1, source_target_pairs={{8,0},{16,8},{24,16},{9,1},{17,9},{25,17},{10,2},{18,10},{26,18},{... | collective-permute-start | bytes 1179656 | tf_op jit(solution)/shard_map/ppermute | solution.py:17
  12.0 128.4 %all-gather.3.cloned.1.call-start = ((), (), s32[]{:S(2)}) async-start(), calls=%async_computation.1 | async-start | bytes 3538944 | tf_op jit(solution)/shard_map/all_gather | solution.py:139
  12.1 10.1 %collective-permute-start = (bf16[48,4096]{1,0:T(8,128)(2,1)S(1)}, bf16[48,4096]{1,0:T(8,128)(2,1)S(1)}, u32[]{:S(2)}, u32[]{:S(2)}) collective-permute-start(bf16[48,4096]{1,0:T(8,128)(2,1)S(1)} %bitcast.151), channel_id=1, source_target_pairs={{0,8},{8,16},{16,24},{1,9},{9,17},{17,25},{2,10},{10,18},{18,26},{... | collective-permute-start | bytes 1179656 | tf_op jit(solution)/shard_map/ppermute | solution.py:17
  23.4 260.5 %reduce-scatter.2.cloned.1.call-start = ((), (), s32[]{:S(2)}) async-start(), calls=%async_computation.3 | async-start | bytes 7077888 | tf_op jit(solution)/shard_map/reduce_scatter | solution.py:149
  42.4 8.8 %copy-start.3 = (bf16[1,384,3,256]{3,1,2,0:T(8,128)(2,1)S(1)}, bf16[1,384,3,256]{3,1,2,0:T(8,128)(2,1)}, u32[]{:S(2)}) copy-start(bf16[1,384,3,256]{3,1,2,0:T(8,128)(2,1)} %param.16) | copy-start | bytes 1769476
  42.4 9.1 %copy-start.9 = (s32[1,2,384]{2,1,0:T(2,128)S(1)}, s32[1,2,384]{2,1,0:T(2,128)}, u32[]{:S(2)}) copy-start(s32[1,2,384]{2,1,0:T(2,128)} %param.21) | copy-start | bytes 9220
  79.0 4.0 %copy-start.2 = (bf16[1,2,256,4096]{3,2,1,0:T(8,128)(2,1)S(1)}, bf16[1,2,256,4096]{3,2,1,0:T(8,128)(2,1)}, u32[]{:S(2)}) copy-start(bf16[1,2,256,4096]{3,2,1,0:T(8,128)(2,1)} %param.19) | copy-start | bytes 12582916
  91.0 56.0 %slice-start.2 = ((s8[6291456]{0:T(1024)(128)(4,1)}), s8[2097152]{0:T(1024)(128)(4,1)S(1)}, s32[]{:S(2)}) async-start(s8[6291456]{0:T(1024)(128)(4,1)} %bitcast.128), calls=%async_computation.6 | async-start | bytes 4194304
  140.5 6.5 %slice-start.3 = ((s8[6291456]{0:T(1024)(128)(4,1)}), s8[4194304]{0:T(1024)(128)(4,1)S(1)}, s32[]{:S(2)}) async-start(s8[6291456]{0:T(1024)(128)(4,1)} %bitcast.128), calls=%async_computation.7 | async-start | bytes 8388608
  140.5 6.5 %copy-start.10 = (bf16[384,4096]{1,0:T(8,128)(2,1)S(1)}, bf16[384,4096]{1,0:T(8,128)(2,1)}, u32[]{:S(2)}) copy-start(bf16[384,4096]{1,0:T(8,128)(2,1)} %all-gather.3.cloned.1.call-done) | copy-start | bytes 9437188
  149.7 0.9 copy-start.6
  152.0 5.9 %slice-start = ((s8[6291456]{0:T(1024)(128)(4,1)}), s8[4194304]{0:T(1024)(128)(4,1)S(1)}, s32[]{:S(2)}) async-start(s8[6291456]{0:T(1024)(128)(4,1)} %bitcast.125), calls=%async_computation.4 | async-start | bytes 8388608
  154.7 3.0 %copy-start.5 = (bf16[384,1,2,128]{0,3,2,1:T(8,128)(2,1)S(1)}, bf16[384,1,2,128]{0,3,2,1:T(8,128)(2,1)}, u32[]{:S(2)}) copy-start(bf16[384,1,2,128]{0,3,2,1:T(8,128)(2,1)} %fusion.32) | copy-start | bytes 589828
  154.8 3.1 %slice-start.1 = ((s8[6291456]{0:T(1024)(128)(4,1)}), s8[2097152]{0:T(1024)(128)(4,1)S(1)}, s32[]{:S(2)}) async-start(s8[6291456]{0:T(1024)(128)(4,1)} %bitcast.125), calls=%async_computation.5 | async-start | bytes 4194304
  157.8 3.0 %slice-start.4 = ((s8[6291456]{0:T(1024)(128)(4,1)}), s8[4194304]{0:T(1024)(128)(4,1)S(1)}, s32[]{:S(2)}) async-start(s8[6291456]{0:T(1024)(128)(4,1)} %bitcast.131), calls=%async_computation.8 | async-start | bytes 8388608
  157.9 2.9 slice-start.5
  167.1 118.1 %copy-start.1 = (bf16[1,48,4096]{2,1,0:T(8,128)(2,1)S(1)}, bf16[1,48,4096]{2,1,0:T(8,128)(2,1)}, u32[]{:S(2)}) copy-start(bf16[1,48,4096]{2,1,0:T(8,128)(2,1)} %param.15) | copy-start | bytes 1179652
  167.2 118.4 %copy-start = (bf16[48,4096]{1,0:T(8,128)(2,1)S(1)}, bf16[48,4096]{1,0:T(8,128)(2,1)}, u32[]{:S(2)}) copy-start(bf16[48,4096]{1,0:T(8,128)(2,1)} %broadcast_select_fusion) | copy-start | bytes 1179652
Sparse Core Ops, SparseCore 0:
  12.1 66.7 all-gather.4
  81.7 58.6 all-gather.2
  167.2 116.6 reduce-scatter.1
where the time goes:
time: 294 us; the launch traced here: 293 us
  waiting for transfers between devices  192 us (65%)
  matrix products  38.1 us (13%)
  local copies, waits for them, and re-layouts  29.1 us (10%)
  between operations  14.2 us (5%)
  starting transfers between devices  10.3 us (4%)
  other arithmetic  9.42 us (3%)
    reduce_scatter x1, waiting for transfers between devices, body(): lax.psum_scatter(jnp.concatenate([forward_piece(first, local * lax.axis_s...  117 us
    all_gather x1, waiting for transfers between devices, body(): lax.all_gather(normed, 'tp', axis=0, tiled=True)  47.1 us
    dot_general x8, matrix products, contract(): lax.dot_general(rows, weights, (((1,), (side,)), ((), ())), preferred_ele...  27.8 us
    all_gather x1, waiting for transfers between devices, body(): lax.all_gather(upstream, 'tp', axis=0, tiled=True)  24.8 us
    unnamed x40, local copies, waits for them, and re-layouts  18.3 us
    ppermute x2, starting transfers between devices, from_behind(): return lax.ppermute(block, axis, route)  10.2 us
    slice x1, local copies, waits for them, and re-layouts, selected(): second = contract(rows, weights[1], side)  10.2 us
  transfers between devices with their start and end apart: 5, of which 5 were waited for; matrix products, arithmetic and copies ran while one was open for 16% of the time, Pallas kernels for 0%

commit v1 on v0

v1 whole, which is shorter than its diff:
```python
import functools
import math

import jax
import jax.numpy as jnp
from jax import lax
from jax.experimental import pallas as pl
from jax.experimental.pallas import tpu as pltpu
from jax.sharding import PartitionSpec as P

HEAD_DIM = 128
EPSILON = 1e-05
NT = (((1,), (1,)), ((), ()))
NN = (((1,), (0,)), ((), ()))
TN = (((0,), (0,)), ((), ()))
F32 = jnp.float32
BF16 = jnp.bfloat16


def dot(a, b, dims):
    return lax.dot_general(a, b, dims, preferred_element_type=F32)


def pick(labels, first, second):
    return jnp.where(jnp.broadcast_to(labels, first.shape) == 0, first, second)


def kernel(
    n,
    sections,
    emb,
    prev,
    top,
    gout,
    saved_in,
    sqkv,
    gain,
    wq,
    wo,
    meta,
    docs,
    out_f,
    out_b,
    wq_v,
    wo_v,
    arrived,
    returned,
    xin,
    ag,
    part,
    rs,
    acc,
    pr,
    att,
    grads,
    w_sem,
    sec_send,
    sec_recv,
    ag_send,
    ag_recv,
    rs_send,
    rs_recv,
):
    half = n // 2
    local, width = emb.shape
    cols = width // 2
    length = n * local
    hw = wo.shape[1]
    heads = hw // HEAD_DIM
    scale = 1.0 / math.sqrt(HEAD_DIM)
    section = lax.axis_index("section")
    me = lax.axis_index("tp")
    odd = me % 2
    pos = (1 - odd) * (me // 2) + odd * (n - 1 - me // 2)

    def member(p):
        q = (p + 2 * n) % n
        upper = q // half
        return (1 - upper) * 2 * q + upper * (2 * (n - q) - 1)

    neighbours = ({"tp": member(pos + 1)}, {"tp": member(pos - 1)})
    after = {"section": (section + 1) % sections}
    before = {"section": (section + sections - 1) % sections}

    w_copies = [
        pltpu.make_async_copy(wq, wq_v, w_sem.at[0]),
        pltpu.make_async_copy(wo, wo_v, w_sem.at[1]),
    ]
    for c in w_copies:
        c.start()

    barrier = pltpu.get_barrier_semaphore()
    for device in (*neighbours, after, before):
        pl.semaphore_signal(
            barrier, inc=1, device_id=device, device_id_type=pl.DeviceIdType.MESH
        )
    pl.semaphore_wait(barrier, 4)

    def remote(src, dst, send, recv, device):
        return pltpu.make_async_remote_copy(
            src_ref=src,
            dst_ref=dst,
            send_sem=send,
            recv_sem=recv,
            device_id=device,
            device_id_type=pl.DeviceIdType.MESH,
        )

    hand_f = remote(prev, arrived, sec_send.at[0], sec_recv.at[0], after)
    hand_b = remote(gout, returned, sec_send.at[1], sec_recv.at[1], before)
    hand_f.start()
    hand_b.start()
    sent = []

    def chunk(c):
        return pl.ds(c * cols, cols)

    def ag_chunks(d, k):
        return (0, 1) if k < half else (d,)

    def ag_copy(p, d, k, c):
        sign = 1 - 2 * d
        block = ag.at[p, member(pos - sign * (k - 1)), :, chunk(c)]
        return remote(
            block, block, ag_send.at[p, d, k - 1, c], ag_recv.at[p, d, k - 1, c], neighbours[d]
        )

    def ag_step(p, k):
        for c in range(2):
            for d in range(2):
                if k > 1 and c in ag_chunks(d, k - 1):
                    ag_copy(p, d, k - 1, c).wait_recv()
                if k <= half and c in ag_chunks(d, k):
                    copy = ag_copy(p, d, k, c)
                    copy.start()
                    sent.append(copy)

    def rs_chunks(d, k):
        return (0, 1) if k > 1 else (d,)

    def rs_copy(p, d, k, c):
        sign = 1 - 2 * d
        if k > 1 and c in rs_chunks(d, k - 1):
            src = rs.at[p, d, k - 2, :, chunk(c)]
        else:
            src = part.at[p, member(pos + sign * (half + 1 - k)), :, chunk(c)]
        dst = rs.at[p, d, k - 1, :, chunk(c)]
        return remote(
            src, dst, rs_send.at[p, d, k - 1, c], rs_recv.at[p, d, k - 1, c], neighbours[d]
        )

    def rs_step(p, k):
        for c in range(2):
            for d in range(2):
                sign = 1 - 2 * d
                if k > 1 and c in rs_chunks(d, k - 1):
                    rs_copy(p, d, k - 1, c).wait_recv()
                    if k <= half:
                        own = part[p, member(pos + sign * (half + 1 - k)), :, chunk(c)]
                        here = rs[p, d, k - 2, :, chunk(c)]
                        rs[p, d, k - 2, :, chunk(c)] = (
                            here.astype(F32) + own.astype(F32)
                        ).astype(BF16)
                if k <= half and c in rs_chunks(d, k):
                    copy = rs_copy(p, d, k, c)
                    copy.start()
                    sent.append(copy)

    def rs_total(p):
        return (
            part[p, me].astype(F32)
            + rs[p, 0, half - 1].astype(F32)
            + rs[p, 1, half - 1].astype(F32)
        )

    def own_labels(col):
        return meta[pl.ds(pl.multiple_of(me * local, 8), local), col : col + 1]

    def gains(col):
        labels = jnp.broadcast_to(own_labels(col), (local, width))
        return jnp.where(labels == 0, gain[0:1, :], gain[1:2, :])

    def probabilities(queries, keys, which):
        scores = dot(queries, keys, NT) * scale
        row = lax.broadcasted_iota(jnp.int32, (length, length), 0)
        column = lax.broadcasted_iota(jnp.int32, (length, length), 1)
        allowed = (column <= row) & (meta[:, 2 + which : 3 + which] == docs[which : which + 1, :])
        scores = jnp.where(allowed, scores, -jnp.inf)
        weights = jnp.exp(scores - jnp.max(scores, axis=-1, keepdims=True))
        return weights / jnp.sum(weights, axis=-1, keepdims=True)

    depth = min(1024, width)

    def project(p, weights, dims):
        acc[...] = jnp.zeros_like(acc)

        def step(i, carry):
            at = pl.ds(pl.multiple_of(i * depth, depth), depth)
            rows = ag[p, :, :, at].reshape(length, depth)
            for m in range(2):
                acc[m] += dot(rows, weights(m, at), dims)
            return carry

        lax.fori_loop(0, width // depth, step, 0)
        return pick(meta[:, p : p + 1], acc[0], acc[1]).astype(BF16)

    def project_qkv(j):
        pr[j] = project(0, lambda m, at: wq_v[m, j, at, :], NN)

    def attend():
        for h in range(heads):
            at = pl.ds(h * HEAD_DIM, HEAD_DIM)
            probs = probabilities(pr[0, :, at], pr[1, :, at], 0).astype(BF16)
            att[:, at] = dot(probs, pr[2, :, at], NN).astype(BF16)

    tile = 256

    def spread(p, term, first, last):
        def step(i, carry):
            at = pl.ds(pl.multiple_of(i * tile, tile), tile)
            both = [term(m, at) for m in range(2)]
            block = pick(meta[:, p : p + 1], *both).astype(BF16)
            part[p, :, :, at] = block.reshape(n, local, tile)
            return carry

        lax.fori_loop(first, last, step, 0)

    def forward_terms():
        spread(0, lambda m, at: dot(att[...], wo_v[m, :, at], NN), 0, width // tile)

    def backward_term(m, at):
        total = dot(grads[0], wq_v[m, 0, at, :], NT)
        for j in (1, 2):
            total += dot(grads[j], wq_v[m, j, at, :], NT)
        return total

    def backward_terms(first, last):
        spread(1, backward_term, first, last)

    def grad_attended():
        att[...] = project(1, lambda m, at: wo_v[m, :, at], NT)

    def backward_head(h):
        at = pl.ds(h * HEAD_DIM, HEAD_DIM)
        queries, keys, values = (sqkv[j, :, at] for j in range(3))
        upstream = att[:, at]
        probs = probabilities(queries, keys, 1)
        grads[2, :, at] = dot(probs.astype(BF16), upstream, TN).astype(BF16)
        grad_probs = dot(upstream, values, NT)
        delta = jnp.sum(probs * grad_probs, axis=-1, keepdims=True)
        grad_scores = (probs * (grad_probs - delta) * scale).astype(BF16)
        grads[0, :, at] = dot(grad_scores, keys, NN).astype(BF16)
        grads[1, :, at] = dot(grad_scores, queries, TN).astype(BF16)

    def interleave(pieces, steps):
        done = 0
        for i, piece in enumerate(pieces):
            piece()
            due = (i + 1) * len(steps) // len(pieces)
            for s in steps[done:due]:
                s()
            done = due

    hand_f.wait_recv()
    rows = jnp.where(section == 0, emb[...], arrived[...])
    xin[...] = rows
    rows = rows.astype(F32)
    inverse = lax.rsqrt(jnp.mean(rows * rows, axis=-1, keepdims=True) + EPSILON)
    ag[0, me] = (rows * inverse * gains(0)).astype(BF16)
    ag_step(0, 1)
    hand_b.wait_recv()
    ag[1, me] = jnp.where(section == sections - 1, top[...], returned[...])
    for k in range(2, half + 1):
        ag_step(0, k)
    ag_step(1, 1)
    ag_step(0, half + 1)
    for c in w_copies:
        c.wait()

    interleave(
        [functools.partial(project_qkv, j) for j in range(3)] + [attend, forward_terms],
        [functools.partial(ag_step, 1, k) for k in range(2, half + 1)],
    )
    rs_step(0, 1)
    ag_step(1, half + 1)
    tiles = width // tile
    interleave(
        [grad_attended]
        + [functools.partial(backward_head, h) for h in range(heads)]
        + [
            functools.partial(backward_terms, 0, tiles // 2),
            functools.partial(backward_terms, tiles // 2, tiles),
        ],
        [functools.partial(rs_step, 0, k) for k in range(2, half + 1)],
    )
    rs_step(1, 1)
    rs_step(0, half + 1)
    out_f[...] = (xin[...].astype(F32) + rs_total(0)).astype(BF16)
    for k in range(2, half + 2):
        rs_step(1, k)
    back_rows = saved_in[...].astype(F32)
    inverse = lax.rsqrt(jnp.mean(back_rows * back_rows, axis=-1, keepdims=True) + EPSILON)
    scaled = rs_total(1) * gains(1)
    correction = jnp.mean(scaled * back_rows, axis=-1, keepdims=True)
    norm_grad = inverse * scaled - back_rows * (inverse * inverse * inverse * correction)
    out_b[...] = (ag[1, me].astype(F32) + norm_grad).astype(BF16)

    hand_f.wait_send()
    hand_b.wait_send()
    for copy in sent:
        copy.wait_send()


def body(
    n,
    sections,
    embedded,
    previous_out,
    top_grad,
    grad_out,
    saved_input,
    saved_qkv,
    norm_gain,
    qkv_weight,
    out_weight,
    modality,
    documents,
):
    local, width = embedded.shape
    length = local * n
    hw = out_weight.shape[2]
    half = n // 2
    meta = jnp.concatenate([modality[0], documents[0]], axis=0).T
    vmem = pl.BlockSpec(memory_space=pltpu.VMEM)
    hbm = pl.BlockSpec(memory_space=pl.ANY)
    dma = pltpu.SemaphoreType.DMA
    out = jax.ShapeDtypeStruct((local, width), BF16)
    forward_out, backward_out = pl.pallas_call(
        functools.partial(kernel, n, sections),
        out_shape=(out, out),
        in_specs=[vmem] * 7 + [hbm, hbm] + [vmem] * 2,
        out_specs=(vmem, vmem),
        scratch_shapes=[
            pltpu.VMEM((2, 3, width, hw), BF16),
            pltpu.VMEM((2, hw, width), BF16),
            pltpu.VMEM((local, width), BF16),
            pltpu.VMEM((local, width), BF16),
            pltpu.VMEM((local, width), BF16),
            pltpu.VMEM((2, n, local, width), BF16),
            pltpu.VMEM((2, n, local, width), BF16),
            pltpu.VMEM((2, 2, half, local, width), BF16),
            pltpu.VMEM((2, length, hw), F32),
            pltpu.VMEM((3, length, hw), BF16),
            pltpu.VMEM((length, hw), BF16),
            pltpu.VMEM((3, length, hw), BF16),
            dma((2,)),
            dma((2,)),
            dma((2,)),
            dma((2, 2, half, 2)),
            dma((2, 2, half, 2)),
            dma((2, 2, half, 2)),
            dma((2, 2, half, 2)),
        ],
        compiler_params=pltpu.CompilerParams(
            collective_id=0, has_side_effects=True, vmem_limit_bytes=64000000
        ),
    )(
        embedded,
        previous_out[0],
        top_grad,
        grad_out[0],
        saved_input[0],
        saved_qkv[0].transpose(1, 0, 2),
        norm_gain[0],
        qkv_weight[0].transpose(0, 2, 1, 3),
        out_weight[0],
        meta,
        documents[0],
    )
    return (forward_out[None], backward_out[None])


def solution(mesh):
    placed = (
        P("tp", None),
        P("section", "tp", None),
        P("tp", None),
        P("section", "tp", None),
        P("section", "tp", None),
        P("section", None, None, "tp"),
        P("section", None, None),
        P("section", None, None, None, "tp"),
        P("section", None, "tp", None),
        P("section", None, None),
        P("section", None, None),
    )
    return jax.shard_map(
        functools.partial(body, mesh.shape["tp"], mesh.shape["section"]),
        mesh=mesh,
        in_specs=placed,
        out_specs=(P("section", "tp", None), P("section", "tp", None)),
        check_vma=False,
    )
```

time: 294 us -> 143 us (0.49)
  waiting for transfers between devices: 192 us -> 0 us
  Pallas kernels: 0 us -> 137 us
  matrix products: 38.1 us -> 0 us
  local copies, waits for them, and re-layouts: 29.1 us -> 4.36 us
  between operations: 14.2 us -> 0.64 us
  starting transfers between devices: 10.3 us -> 0 us
  other arithmetic: 9.42 us -> 0.71 us
    pallas_call x0 -> x1, Pallas kernels: none -> 137 us  [body(): pl.pallas_call(functools.partial(kernel, n, sections), out_shape=(out, ou...]
    reduce_scatter x1 -> x0, waiting for transfers between devices: 117 us -> none  [body(): lax.psum_scatter(jnp.concatenate([forward_piece(first, local * lax.axis_s...]
    all_gather x2 -> x0, waiting for transfers between devices: 71.9 us -> none  [the longest x1 47.1 us: body(): lax.all_gather(normed, 'tp', axis=0, tiled=True)]
    dot_general x13 -> x0, matrix products: 35.8 us -> none  [the longest x8 27.8 us: contract(): lax.dot_general(rows, weights, (((1,), (side,)), ((), ())), preferred_ele...]
    unnamed x40 -> x2, local copies, waits for them, and re-layouts: 18.3 us -> 3.53 us
    slice x5 -> x0, local copies, waits for them, and re-layouts: 10.6 us -> none  [the longest x1 10.2 us: selected(): second = contract(rows, weights[1], side)]
    ppermute x2 -> x0, starting transfers between devices: 10.2 us -> none  [from_behind(): return lax.ppermute(block, axis, route)]
    ppermute x2 -> x0, waiting for transfers between devices: 3.67 us -> none  [from_behind(): return lax.ppermute(block, axis, route)]
  transfers between devices with their start and end apart: 5 -> 0, of which waited for: 5 -> 0; matrix products, arithmetic and copies ran while one was open for 16% -> 0% of each run, Pallas kernels for 0% -> 0%
where the time goes in v1:
time: 143 us
  Pallas kernels  137 us (96%)
  local copies, waits for them, and re-layouts  4.36 us (3%)
    pallas_call x1, Pallas kernels, body(): pl.pallas_call(functools.partial(kernel, n, sections), out_shape=(out, ou...  137 us
    unnamed x2, local copies, waits for them, and re-layouts  3.53 us

profile of v1, /device:TPU:0, one launch (start us, length us, event | category | flops | bytes accessed | tf_op | source)
XLA Modules:
  0.0 142.7 jit_solution(15227371155011106563)
XLA Ops:
  0.6 0.7 add_bitcast_fusion
  1.3 0.8 copy.13.meta
  2.2 137.0 %shard_map.122 = (bf16[48,4096]{1,0:T(8,128)(2,1)}, bf16[48,4096]{1,0:T(8,128)(2,1)}) custom-call(bf16[48,4096]{1,0:T(8,128)(2,1)} %emb.1, bf16[48,4096]{1,0:T(8,128)(2,1)} %bitcast.22, bf16[48,4096]{1,0:T(8,128)(2,1)} %top.1, bf16[48,4096]{1,0:T(8,128)(2,1)} %bitcast.23, bf16[48,4096]{1,0:T(8,128)(2,1)} %bitcast.24, bf16[3,384,256]{2,1,0:T(8,128)(2,1)} %bitcast.19, ...), custom_call_target="tpu_custom_call" | custom-call | tf_op jit(solution)/shard_map/pallas_call | solution.py:338
  139.1 1.8 %copy.16 = bf16[1,48,4096]{2,1,0:T(8,128)(2,1)} copy(bf16[1,48,4096]{2,1,0:T(8,128)(2,1)} %bitcast.21) | data formatting | bytes 786432
  140.9 1.8 %copy.17 = bf16[1,48,4096]{2,1,0:T(8,128)(2,1)} copy(bf16[1,48,4096]{2,1,0:T(8,128)(2,1)} %bitcast.20) | data formatting | bytes 786432

commit v2 on v1

--- a/solution.py
+++ b/solution.py
@@ -15,6 +15,7 @@
 TN = (((0,), (0,)), ((), ()))
 F32 = jnp.float32
 BF16 = jnp.bfloat16
+CHUNKS = 4
 
 
 def dot(a, b, dims):
@@ -37,10 +38,9 @@
     gain,
     wq,
     wo,
-    meta,
+    labels,
     docs,
-    out_f,
-    out_b,
+    out,
     wq_v,
     wo_v,
     arrived,
@@ -53,6 +53,7 @@
     pr,
     att,
     grads,
+    meta,
     w_sem,
     sec_send,
     sec_recv,
@@ -63,7 +64,7 @@
 ):
     half = n // 2
     local, width = emb.shape
-    cols = width // 2
+    cols = width // CHUNKS
     length = n * local
     hw = wo.shape[1]
     heads = hw // HEAD_DIM
@@ -81,6 +82,8 @@
     neighbours = ({"tp": member(pos + 1)}, {"tp": member(pos - 1)})
     after = {"section": (section + 1) % sections}
     before = {"section": (section + sections - 1) % sections}
+    has_after = section < sections - 1
+    has_before = section > 0
 
     w_copies = [
         pltpu.make_async_copy(wq, wq_v, w_sem.at[0]),
@@ -108,15 +111,30 @@
 
     hand_f = remote(prev, arrived, sec_send.at[0], sec_recv.at[0], after)
     hand_b = remote(gout, returned, sec_send.at[1], sec_recv.at[1], before)
-    hand_f.start()
-    hand_b.start()
+
+    @pl.when(has_after)
+    def _():
+        hand_f.start()
+
+    @pl.when(has_before)
+    def _():
+        hand_b.start()
+
+    line = lax.broadcasted_iota(jnp.int32, (8, length), 0)
+    stacked = jnp.broadcast_to(docs[1:2, :], (8, length))
+    for i, row in ((2, docs[0:1, :]), (1, labels[1:2, :]), (0, labels[0:1, :])):
+        stacked = jnp.where(line == i, jnp.broadcast_to(row, (8, length)), stacked)
+    meta[...] = stacked.T
     sent = []
 
     def chunk(c):
         return pl.ds(c * cols, cols)
 
+    def side(d):
+        return range(d * CHUNKS // 2, (d + 1) * CHUNKS // 2)
+
     def ag_chunks(d, k):
-        return (0, 1) if k < half else (d,)
+        return range(CHUNKS) if k < half else side(d)
 
     def ag_copy(p, d, k, c):
         sign = 1 - 2 * d
@@ -126,7 +144,7 @@
         )
 
     def ag_step(p, k):
-        for c in range(2):
+        for c in range(CHUNKS):
             for d in range(2):
                 if k > 1 and c in ag_chunks(d, k - 1):
                     ag_copy(p, d, k - 1, c).wait_recv()
@@ -136,7 +154,7 @@
                     sent.append(copy)
 
     def rs_chunks(d, k):
-        return (0, 1) if k > 1 else (d,)
+        return range(CHUNKS) if k > 1 else side(d)
 
     def rs_copy(p, d, k, c):
         sign = 1 - 2 * d
@@ -149,22 +167,33 @@
             src, dst, rs_send.at[p, d, k - 1, c], rs_recv.at[p, d, k - 1, c], neighbours[d]
         )
 
+    def rs_start(p, d, k, c):
+        copy = rs_copy(p, d, k, c)
+        copy.start()
+        sent.append(copy)
+
+    def rs_begin(p):
+        for k in (1, 2):
+            for i in range(CHUNKS // 2):
+                for d in range(2):
+                    rs_start(p, d, k, side(d if k == 1 else 1 - d)[i])
+
     def rs_step(p, k):
-        for c in range(2):
+        for i in range(CHUNKS):
             for d in range(2):
+                order = [*side(d), *side(1 - d)]
+                c = order[i]
+                if c not in rs_chunks(d, k - 1):
+                    continue
                 sign = 1 - 2 * d
-                if k > 1 and c in rs_chunks(d, k - 1):
-                    rs_copy(p, d, k - 1, c).wait_recv()
-                    if k <= half:
-                        own = part[p, member(pos + sign * (half + 1 - k)), :, chunk(c)]
-                        here = rs[p, d, k - 2, :, chunk(c)]
-                        rs[p, d, k - 2, :, chunk(c)] = (
-                            here.astype(F32) + own.astype(F32)
-                        ).astype(BF16)
-                if k <= half and c in rs_chunks(d, k):
-                    copy = rs_copy(p, d, k, c)
-                    copy.start()
-                    sent.append(copy)
+                rs_copy(p, d, k - 1, c).wait_recv()
+                if k <= half:
+                    own = part[p, member(pos + sign * (half + 1 - k)), :, chunk(c)]
+                    here = rs[p, d, k - 2, :, chunk(c)]
+                    rs[p, d, k - 2, :, chunk(c)] = (
+                        here.astype(F32) + own.astype(F32)
+                    ).astype(BF16)
+                    rs_start(p, d, k, c)
 
     def rs_total(p):
         return (
@@ -177,8 +206,8 @@
         return meta[pl.ds(pl.multiple_of(me * local, 8), local), col : col + 1]
 
     def gains(col):
-        labels = jnp.broadcast_to(own_labels(col), (local, width))
-        return jnp.where(labels == 0, gain[0:1, :], gain[1:2, :])
+        own = jnp.broadcast_to(own_labels(col), (local, width))
+        return jnp.where(own == 0, gain[0:1, :], gain[1:2, :])
 
     def probabilities(queries, keys, which):
         scores = dot(queries, keys, NT) * scale
@@ -261,15 +290,30 @@
                 s()
             done = due
 
-    hand_f.wait_recv()
-    rows = jnp.where(section == 0, emb[...], arrived[...])
-    xin[...] = rows
+    @pl.when(has_before)
+    def _():
+        hand_f.wait_recv()
+        xin[...] = arrived[...]
+
+    @pl.when(section == 0)
+    def _():
+        xin[...] = emb[...]
+
+    rows = xin[...]
     rows = rows.astype(F32)
     inverse = lax.rsqrt(jnp.mean(rows * rows, axis=-1, keepdims=True) + EPSILON)
     ag[0, me] = (rows * inverse * gains(0)).astype(BF16)
     ag_step(0, 1)
-    hand_b.wait_recv()
-    ag[1, me] = jnp.where(section == sections - 1, top[...], returned[...])
+
+    @pl.when(has_after)
+    def _():
+        hand_b.wait_recv()
+        ag[1, me] = returned[...]
+
+    @pl.when(section == sections - 1)
+    def _():
+        ag[1, me] = top[...]
+
     for k in range(2, half + 1):
         ag_step(0, k)
     ag_step(1, 1)
@@ -281,7 +325,7 @@
         [functools.partial(project_qkv, j) for j in range(3)] + [attend, forward_terms],
         [functools.partial(ag_step, 1, k) for k in range(2, half + 1)],
     )
-    rs_step(0, 1)
+    rs_begin(0)
     ag_step(1, half + 1)
     tiles = width // tile
     interleave(
@@ -293,20 +337,27 @@
         ],
         [functools.partial(rs_step, 0, k) for k in range(2, half + 1)],
     )
-    rs_step(1, 1)
+    rs_begin(1)
     rs_step(0, half + 1)
-    out_f[...] = (xin[...].astype(F32) + rs_total(0)).astype(BF16)
-    for k in range(2, half + 2):
+    out[0] = (xin[...].astype(F32) + rs_total(0)).astype(BF16)
+    for k in range(2, half + 1):
         rs_step(1, k)
     back_rows = saved_in[...].astype(F32)
     inverse = lax.rsqrt(jnp.mean(back_rows * back_rows, axis=-1, keepdims=True) + EPSILON)
+    rs_step(1, half + 1)
     scaled = rs_total(1) * gains(1)
     correction = jnp.mean(scaled * back_rows, axis=-1, keepdims=True)
     norm_grad = inverse * scaled - back_rows * (inverse * inverse * inverse * correction)
-    out_b[...] = (ag[1, me].astype(F32) + norm_grad).astype(BF16)
-
-    hand_f.wait_send()
-    hand_b.wait_send()
+    out[1] = (ag[1, me].astype(F32) + norm_grad).astype(BF16)
+
+    @pl.when(has_after)
+    def _():
+        hand_f.wait_send()
+
+    @pl.when(has_before)
+    def _():
+        hand_b.wait_send()
+
     for copy in sent:
         copy.wait_send()
 
@@ -330,16 +381,15 @@
     length = local * n
     hw = out_weight.shape[2]
     half = n // 2
-    meta = jnp.concatenate([modality[0], documents[0]], axis=0).T
     vmem = pl.BlockSpec(memory_space=pltpu.VMEM)
     hbm = pl.BlockSpec(memory_space=pl.ANY)
     dma = pltpu.SemaphoreType.DMA
-    out = jax.ShapeDtypeStruct((local, width), BF16)
-    forward_out, backward_out = pl.pallas_call(
+    out = jax.ShapeDtypeStruct((2, local, width), BF16)
+    both = pl.pallas_call(
         functools.partial(kernel, n, sections),
-        out_shape=(out, out),
+        out_shape=out,
         in_specs=[vmem] * 7 + [hbm, hbm] + [vmem] * 2,
-        out_specs=(vmem, vmem),
+        out_specs=vmem,
         scratch_shapes=[
             pltpu.VMEM((2, 3, width, hw), BF16),
             pltpu.VMEM((2, hw, width), BF16),
@@ -353,13 +403,14 @@
             pltpu.VMEM((3, length, hw), BF16),
             pltpu.VMEM((length, hw), BF16),
             pltpu.VMEM((3, length, hw), BF16),
+            pltpu.VMEM((length, 8), jnp.int32),
             dma((2,)),
             dma((2,)),
             dma((2,)),
-            dma((2, 2, half, 2)),
-            dma((2, 2, half, 2)),
-            dma((2, 2, half, 2)),
-            dma((2, 2, half, 2)),
+            dma((2, 2, half, CHUNKS)),
+            dma((2, 2, half, CHUNKS)),
+            dma((2, 2, half, CHUNKS)),
+            dma((2, 2, half, CHUNKS)),
         ],
         compiler_params=pltpu.CompilerParams(
             collective_id=0, has_side_effects=True, vmem_limit_bytes=64000000
@@ -374,10 +425,10 @@
         norm_gain[0],
         qkv_weight[0].transpose(0, 2, 1, 3),
         out_weight[0],
-        meta,
+        modality[0],
         documents[0],
     )
-    return (forward_out[None], backward_out[None])
+    return (both[0:1], both[1:2])
 
 
 def solution(mesh):

time: 143 us -> 134 us (0.937)
  Pallas kernels: 137 us -> 132 us
  local copies, waits for them, and re-layouts: 4.36 us -> 2.04 us
    pallas_call x1, Pallas kernels: 137 us -> 132 us  [body(): pl.pallas_call(functools.partial(kernel, n, sections), out_shape=out, in_...]
    unnamed x2 -> x0, local copies, waits for them, and re-layouts: 3.53 us -> none
    slice x0 -> x1, local copies, waits for them, and re-layouts: none -> 2.04 us  [body(): return (both[0:1], both[1:2])]
where the time goes in v2:
time: 134 us
  Pallas kernels  132 us (99%)
  local copies, waits for them, and re-layouts  2.04 us (2%)
    pallas_call x1, Pallas kernels, body(): pl.pallas_call(functools.partial(kernel, n, sections), out_shape=out, in_...  132 us

profile of v2, /device:TPU:0, one launch (start us, length us, event | category | flops | bytes accessed | tf_op | source)
XLA Modules:
  0.0 134.2 jit_solution(3328631460116525169)
XLA Ops:
  0.6 131.5 %shard_map.122 = bf16[2,48,4096]{2,1,0:T(8,128)(2,1)} custom-call(bf16[48,4096]{1,0:T(8,128)(2,1)} %emb.1, bf16[48,4096]{1,0:T(8,128)(2,1)} %bitcast.16, bf16[48,4096]{1,0:T(8,128)(2,1)} %top.1, bf16[48,4096]{1,0:T(8,128)(2,1)} %bitcast.17, bf16[48,4096]{1,0:T(8,128)(2,1)} %bitcast.18, bf16[3,384,256]{2,1,0:T(8,128)(2,1)} %bitcast.15, f32[2,4096]{1,0:T(2,128)} %bitcast.19, ...), custom_call_target="tpu_custom_call" | custom-call | tf_op jit(solution)/shard_map/pallas_call | solution.py:388
  132.2 2.0 %fusion = (bf16[1,48,4096]{2,1,0:T(8,128)(2,1)}, bf16[1,48,4096]{2,1,0:T(8,128)(2,1)}) fusion(bf16[2,48,4096]{2,1,0:T(8,128)(2,1)} %shard_map.122), kind=kLoop, calls=%fused_computation | loop fusion | bytes 1572864 | tf_op jit(solution)/shard_map/slice | solution.py:431
